TPU v7x, 32 devices: a whole 2x2x4 slice. The times are simulated.
32 devices in a mesh: gx: 4 (over z), gy: 8 (over y, x, core).
Axes of the slice: x: 2, y: 2, z: 4, core: 2. Of those that a mesh axis runs over, the one named last changes fastest.
Arguments:
- tokens: bfloat16 [2048, 6144], P('gy', 'gx'), may hold values from -7.5 to 7.5, as said below
- norm_gain: float32 [6144], P('gx'), may hold values from 0.1 to 1.9
- joined_weight: bfloat16 [6144, 43008], P('gx', 'gy'), may hold values from -0.078125 to 0.078125
Outputs:
- projected: bfloat16 [256, 8, 43008], P('gx', None, 'gy')
Inputs may be any that keep to these rules, and one draw needn't show every extreme that they name: Every entry of tokens lies between -7.5 and 7.5; each token's features are noise plus an offset of its own plus a slope of its own times a ramp from -1 to 1 over the 6144 features.
All inputs are finite; a program needn't handle non-finite values.
Results may differ from a plain program's by a relative error of at most 0.014.
Values may be sent and summed in bfloat16 or wider, within the bound.
A program may use at most 128 MiB of HBM per device.

v0:
```python
import functools

import jax
import jax.numpy as jnp
from jax import lax
from jax.experimental import pallas as pl
from jax.experimental.pallas import tpu as pltpu
from jax.sharding import PartitionSpec as P

MESH = pl.DeviceIdType.MESH
EPSILON = 1e-06
SKEW = 1
STAGES = 4


def partner(y, step, ny):
    out, bit = 0, 1
    while bit < ny:
        out = out + bit * ((y // bit + step // bit) % 2)
        bit *= 2
    return out


def kernel(n, ny, width, tok_ref, gain_ref, w_hbm, out_hbm, w_s, gat, stat, recv, acc, stg, ostg,
           cen, coef, gw, fin, tok_sem, w_sem, stat_send, stat_recv, gw_send, gw_recv, gat_send, gat_recv, send_sem, recv_sem, out_sem):
    z, y = lax.axis_index("gx"), lax.axis_index("gy")
    tok, depth = tok_ref.shape
    part = tok // n
    stages = stg.shape[0]
    columns = w_hbm.shape[1]
    tiles = columns // width
    chunks = ny * tiles
    last_lag = SKEW * (n - 1) + 1
    ring = last_lag + 1
    model = depth * n

    def cols(tile):
        if tiles == 1:
            return slice(None)
        return pl.ds(pl.multiple_of(tile * width, 128), width)

    def w_copy(tile):
        return pltpu.make_async_copy(w_hbm.at[:, cols(tile)], w_s.at[tile], w_sem.at[tile])

    tok_copy = pltpu.make_async_copy(tok_ref, gat.at[0], tok_sem)
    tok_copy.start()
    for tile in range(tiles):
        w_copy(tile).start()

    barrier = pltpu.get_barrier_semaphore()
    for k in range(1, n):
        pl.semaphore_signal(barrier, inc=1, device_id=((z + k) % n, y), device_id_type=MESH)
    for k in range(1, ny):
        pl.semaphore_signal(barrier, inc=1, device_id=(z, partner(y, k, ny)), device_id_type=MESH)

    tok_copy.wait()
    values = gat[0].astype(jnp.float32)
    total = jnp.sum(values, axis=1, keepdims=True)
    off = values - total / depth
    squares = jnp.sum(off * off, axis=1, keepdims=True)
    lane = lax.broadcasted_iota(jnp.int32, (tok, 128), 1)
    packed = jnp.where(lane == 0, total, squares)
    stat[z] = packed.T[:8]

    cen[...] = (off * gain_ref[...]).astype(jnp.bfloat16)
    w_copy(0).wait()
    acc[0] = jnp.dot(cen[...], w_s[0], preferred_element_type=jnp.float32).astype(jnp.bfloat16)

    pl.semaphore_wait(barrier, n - 1 + ny - 1)

    def across(ref, send, get, k, slot):
        return pltpu.make_async_remote_copy(
            src_ref=ref.at[slot], dst_ref=ref.at[slot], send_sem=send.at[k], recv_sem=get.at[k],
            device_id=((z + k) % n, y), device_id_type=MESH)

    def gat_copy(k):
        return pltpu.make_async_remote_copy(
            src_ref=gat.at[0], dst_ref=gat.at[k], send_sem=gat_send.at[k], recv_sem=gat_recv.at[k],
            device_id=(z, partner(y, k, ny)), device_id_type=MESH)

    def z_copy(stage, index, slot, chunk, to):
        return pltpu.make_async_remote_copy(
            src_ref=stg.at[stage, index], dst_ref=recv.at[slot, chunk], send_sem=send_sem.at[stage, index],
            recv_sem=recv_sem.at[slot, chunk], device_id=(to, y), device_id_type=MESH)

    def arrived(slot, chunk):
        pltpu.make_async_remote_copy(
            src_ref=recv.at[slot, chunk], dst_ref=recv.at[slot, chunk], send_sem=send_sem.at[0, 0],
            recv_sem=recv_sem.at[slot, chunk], device_id=((z + 1) % n, y), device_id_type=MESH).wait_recv()

    def rows(plane):
        return pl.ds(pl.multiple_of(plane * part, part), part)

    def out_copy(chunk):
        token_block = partner(y, chunk // tiles, ny)
        return pltpu.make_async_copy(
            ostg.at[chunk % 2], out_hbm.at[token_block, :, cols(chunk % tiles)], out_sem.at[chunk % 2])

    def forward(chunk, plane, index, out_slot, in_slot, first, to):
        stage = chunk % stages

        @pl.when(chunk >= stages)
        def _():
            z_copy(stage, index, out_slot, chunk, to).wait_send()

        @pl.when(first)
        def _():
            stg[stage, index] = acc[chunk % ring, rows(plane), :]

        @pl.when(jnp.logical_not(first))
        def _():
            arrived(in_slot, chunk)
            stg[stage, index] = (
                acc[chunk % ring, rows(plane), :].astype(jnp.float32) + recv[in_slot, chunk].astype(jnp.float32)
            ).astype(jnp.bfloat16)

        z_copy(stage, index, out_slot, chunk, to).start()

    def right_stage(chunk):
        for j in reversed(range(n - 1)):
            @pl.when(z + 1 + j < n)
            def _():
                forward(chunk, z + 1 + j, j, j, j + 1, z == 0, z + 1)

    def left_stage(chunk):
        for j in reversed(range(n - 1)):
            @pl.when(z - 1 - j >= 0)
            def _():
                forward(chunk, z - 1 - j, n - 2 - j, n - j, n - 1 - j, z == n - 1, z - 1)

    for k in range(1, n):
        across(stat, stat_send, stat_recv, k, z).start()

    @pl.when(z == 0)
    def _():
        right_stage(jnp.int32(0))

    @pl.when(z == n - 1)
    def _():
        left_stage(jnp.int32(0))

    for k in range(1, n):
        across(stat, stat_send, stat_recv, k, (z + n - k) % n).wait_recv()
    sums = [stat[k, 0:1, :] for k in range(n)]
    mean = functools.reduce(lambda a, b: a + b, sums) / model
    spread = jnp.zeros_like(mean)
    for k in range(n):
        shift = sums[k] / depth - mean
        spread = spread + stat[k, 1:2, :] + depth * shift * shift
    rstd = lax.rsqrt(spread / model + EPSILON)
    line = lax.broadcasted_iota(jnp.int32, (128, tok), 0)
    table = jnp.where(line == n, rstd, mean)
    for k in range(n):
        table = jnp.where(line == k, (sums[k] / depth - mean) * rstd, table)
    coef[...] = table.T
    gat[0] = (
        (gat[0].astype(jnp.float32) - coef[:, n + 1:n + 2]) * coef[:, n:n + 1] * gain_ref[...]
    ).astype(jnp.bfloat16)
    for k in range(1, ny):
        gat_copy(k).start()

    @pl.loop(1, chunks + last_lag)
    def _(it):
        @pl.when(it < chunks)
        def _():
            tile, group = it % tiles, it // tiles

            @pl.when(group == 0)
            def _():
                w_copy(tile).wait()

            @pl.when(jnp.logical_and(group > 0, tile == 0))
            def _():
                gat_copy(group).wait_recv()

            acc[it % ring] = jnp.dot(gat[group], w_s[tile], preferred_element_type=jnp.float32).astype(jnp.bfloat16)

        right = it - SKEW * z

        @pl.when(jnp.logical_and(right >= 0, right < chunks))
        def _():
            right_stage(right)

        left = it - SKEW * (n - 1 - z)

        @pl.when(jnp.logical_and(left >= 0, left < chunks))
        def _():
            left_stage(left)

        @pl.when(it == 1)
        def _():
            gain = gain_ref[...]
            high = gain.astype(jnp.bfloat16).astype(jnp.float32)
            term = lax.broadcasted_iota(jnp.int32, (16, depth), 0)
            pair = jnp.where(term == 0, high, jnp.where(term == 1, gain - high, 0.0)).astype(jnp.bfloat16)
            both = jnp.dot(pair, w_s[0], preferred_element_type=jnp.float32)
            gw[z] = both[0:1] + both[1:2]
            for k in range(1, n):
                across(gw, gw_send, gw_recv, k, z).start()

        own = it - last_lag

        @pl.when(own == 0)
        def _():
            fin[...] = acc[0, rows(z), :].astype(jnp.float32)

            @pl.when(z > 0)
            def _():
                arrived(0, 0)
                fin[...] += recv[0, 0].astype(jnp.float32)

            @pl.when(z < n - 1)
            def _():
                arrived(n, 0)
                fin[...] += recv[n, 0].astype(jnp.float32)

            for k in range(1, n):
                across(gw, gw_send, gw_recv, k, (z + n - k) % n).wait_recv()
            mine = coef[rows(z), :]
            value = fin[...] * mine[:, n:n + 1]
            for k in range(n):
                value = value + mine[:, k:k + 1] * gw[k]
            ostg[0] = value.astype(jnp.bfloat16)
            out_copy(own).start()

        @pl.when(own >= 1)
        def _():
            @pl.when(own >= 2)
            def _():
                out_copy(own - 2).wait()

            mine = acc[own % ring, rows(z), :].astype(jnp.float32)

            @pl.when(z == 0)
            def _():
                arrived(n, own)
                ostg[own % 2] = (mine + recv[n, own].astype(jnp.float32)).astype(jnp.bfloat16)

            @pl.when(z == n - 1)
            def _():
                arrived(0, own)
                ostg[own % 2] = (mine + recv[0, own].astype(jnp.float32)).astype(jnp.bfloat16)

            @pl.when(jnp.logical_and(z > 0, z < n - 1))
            def _():
                arrived(0, own)
                arrived(n, own)
                ostg[own % 2] = (
                    mine + recv[0, own].astype(jnp.float32) + recv[n, own].astype(jnp.float32)
                ).astype(jnp.bfloat16)

            out_copy(own).start()

    for chunk in range(chunks - 2, chunks):
        out_copy(chunk).wait()
    for chunk in range(chunks - stages, chunks):
        for index in range(n - 1):
            z_copy(chunk % stages, index, 0, chunk, (z + 1) % n).wait_send()
    for k in range(1, n):
        across(stat, stat_send, stat_recv, k, z).wait_send()
        across(gw, gw_send, gw_recv, k, z).wait_send()
    for k in range(1, ny):
        gat_copy(k).wait_send()


def reorder_kernel(in_ref, out_ref, take):
    ny, block, width = in_ref.shape
    size = ny * block

    @pl.when(jnp.logical_and(pl.program_id(0) == 0, pl.program_id(1) == 0))
    def _():
        row = lax.broadcasted_iota(jnp.int32, (size, size), 0)
        col = lax.broadcasted_iota(jnp.int32, (size, size), 1)
        take[...] = (col == (row % ny) * block + row // ny).astype(jnp.bfloat16)

    moved = jnp.dot(take[...], in_ref[...].reshape(size, width), preferred_element_type=jnp.float32)
    out_ref[...] = moved.astype(jnp.bfloat16)


def reorder(blocks):
    ny, part, columns = blocks.shape
    block = min(part, max(16, 256 // ny))
    width = tile_width(columns, 14)
    moved = pl.pallas_call(
        reorder_kernel,
        grid=(part // block, columns // width),
        out_shape=jax.ShapeDtypeStruct((part * ny, columns), jnp.bfloat16),
        in_specs=[pl.BlockSpec((ny, block, width), lambda i, j: (0, i, j))],
        out_specs=pl.BlockSpec((block * ny, width), lambda i, j: (i, j)),
        scratch_shapes=[pltpu.VMEM((block * ny, block * ny), jnp.bfloat16)],
        compiler_params=pltpu.CompilerParams(vmem_limit_bytes=67043328),
    )(blocks)
    return moved.reshape(part, ny, columns)


def tile_width(columns, most=7):
    if columns % 128:
        return columns
    lanes = columns // 128
    return 128 * max(k for k in range(1, most + 1) if lanes % k == 0)


def solution(mesh):
    n, ny = mesh.shape["gx"], mesh.shape["gy"]

    def body(tokens, norm_gain, joined_weight):
        tok, depth = tokens.shape
        columns = joined_weight.shape[1]
        part, width = tok // n, tile_width(columns)
        tiles = columns // width
        chunks = ny * tiles
        ring = SKEW * (n - 1) + 2
        stages = STAGES if tiles > 1 else STAGES - 1
        dma = pltpu.SemaphoreType.DMA
        out = pl.pallas_call(
            functools.partial(kernel, n, ny, width),
            out_shape=jax.ShapeDtypeStruct((ny, part, columns), jnp.bfloat16),
            in_specs=[
                pl.BlockSpec(memory_space=pl.ANY),
                pl.BlockSpec(memory_space=pltpu.VMEM),
                pl.BlockSpec(memory_space=pl.ANY),
            ],
            out_specs=pl.BlockSpec(memory_space=pl.ANY),
            scratch_shapes=[
                pltpu.VMEM((tiles, depth, width), jnp.bfloat16),
                pltpu.VMEM((ny, tok, depth), jnp.bfloat16),
                pltpu.VMEM((n, 8, tok), jnp.float32),
                pltpu.VMEM((n + 1, chunks, part, width), jnp.bfloat16),
                pltpu.VMEM((ring, tok, width), jnp.bfloat16),
                pltpu.VMEM((stages, n - 1, part, width), jnp.bfloat16),
                pltpu.VMEM((2, part, width), jnp.bfloat16),
                pltpu.VMEM((tok, depth), jnp.bfloat16),
                pltpu.VMEM((tok, 128), jnp.float32),
                pltpu.VMEM((n + 8, 1, width), jnp.float32),
                pltpu.VMEM((part, width), jnp.float32),
                dma, dma((tiles,)), dma((n,)), dma((n,)), dma((n,)), dma((n,)),
                dma((ny,)), dma((ny,)),
                dma((stages, n - 1)), dma((n + 1, chunks)), dma((2,)),
            ],
            compiler_params=pltpu.CompilerParams(
                collective_id=0, has_side_effects=True, vmem_limit_bytes=67043328),
        )(tokens, norm_gain.reshape(1, depth), joined_weight)
        return reorder(out)

    return jax.shard_map(
        body,
        mesh=mesh,
        in_specs=(P("gy", "gx"), P("gx"), P("gx", "gy")),
        out_specs=P("gx", None, "gy"),
        check_vma=False,
    )
```

profile of v0, /device:TPU:8, one launch (start us, length us, event | category | flops | bytes accessed | tf_op | source)
XLA Modules:
  0.0 379.5 jit_solution(11875755825304353657)
XLA Ops:
  0.0 1.3 reshape.6.gain_ref
  1.3 370.7 %shard_map.37.in_ref = bf16[8,64,5376]{2,1,0:T(8,128)(2,1)} custom-call(bf16[256,1536]{1,0:T(8,128)(2,1)} %tok_ref.1, f32[1,1536]{1,0:T(1,128)} %reshape.6.gain_ref, bf16[1536,5376]{1,0:T(8,128)(2,1)} %w_hbm.1), custom_call_target="tpu_custom_call" | custom-call | tf_op jit(solution)/shard_map/pallas_call | solution.py:315
  372.0 7.6 %shard_map.38 = bf16[512,5376]{1,0:T(8,128)(2,1)} custom-call(bf16[8,64,5376]{2,1,0:T(8,128)(2,1)} %shard_map.37.in_ref), custom_call_target="tpu_custom_call" | custom-call | tf_op jit(solution)/shard_map/pallas_call | solution.py:284
where the time goes:
time: 384 us; the launch traced here: 380 us
  Pallas kernels  378 us (98%)
    pallas_call x1, Pallas kernels, body(): pl.pallas_call(functools.partial(kernel, n, ny, width), out_shape=jax.Sha...  371 us

commit v1 on v0

v1 whole, which is shorter than its diff:
```python
import functools

import jax
import jax.numpy as jnp
from jax import lax
from jax.experimental import pallas as pl
from jax.experimental.pallas import tpu as pltpu
from jax.sharding import PartitionSpec as P

MESH = pl.DeviceIdType.MESH
EPSILON = 1e-06
STAGES = 4


def partner(y, step, ny):
    out, bit = 0, 1
    while bit < ny:
        out = out + bit * ((y // bit + step // bit) % 2)
        bit *= 2
    return out


def kernel(n, ny, width, tok_ref, gain_hbm, w_hbm, out_ref, w_s, gat, gain_s, stat, recv, acc, stg,
           cen, coef, gw, fin, tok_sem, gain_sem, w_sem, stat_send, stat_recv, gw_send, gw_recv, gat_send, gat_recv,
           send_sem, recv_sem):
    z, y = lax.axis_index("gx"), lax.axis_index("gy")
    tok, depth = tok_ref.shape
    part = tok // n
    stages = stg.shape[0]
    slots = recv.shape[1]
    columns = w_hbm.shape[1]
    tiles = columns // width
    chunks = ny * tiles
    ring = acc.shape[0]
    model = depth * n

    def cols(tile):
        if tiles == 1:
            return slice(None)
        return pl.ds(pl.multiple_of(tile * width, 128), width)

    def w_copy(tile):
        return pltpu.make_async_copy(w_hbm.at[:, cols(tile)], w_s.at[tile], w_sem.at[tile])

    tok_copy = pltpu.make_async_copy(tok_ref, gat.at[0], tok_sem)
    tok_copy.start()
    gain_copy = pltpu.make_async_copy(gain_hbm, gain_s, gain_sem)
    gain_copy.start()
    w_copy(0).start()

    barrier = pltpu.get_barrier_semaphore()
    for k in range(1, n):
        pl.semaphore_signal(barrier, inc=1, device_id=((z + k) % n, y), device_id_type=MESH)
    for k in range(1, ny):
        pl.semaphore_signal(barrier, inc=1, device_id=(z, partner(y, k, ny)), device_id_type=MESH)

    def gain_row():
        return gain_s[...].reshape(1, depth)

    tok_copy.wait()
    values = gat[0].astype(jnp.float32)
    total = jnp.sum(values, axis=1, keepdims=True)
    off = values - total / depth
    squares = jnp.sum(off * off, axis=1, keepdims=True)
    lane = lax.broadcasted_iota(jnp.int32, (tok, 128), 1)
    packed = jnp.where(lane == 0, total, squares)
    stat[z] = packed.T[:8]

    gain_copy.wait()
    cen[...] = (off * gain_row()).astype(jnp.bfloat16)

    pl.semaphore_wait(barrier, n - 1 + ny - 1)

    def across(ref, send, get, k, slot):
        return pltpu.make_async_remote_copy(
            src_ref=ref.at[slot], dst_ref=ref.at[slot], send_sem=send.at[k], recv_sem=get.at[k],
            device_id=((z + k) % n, y), device_id_type=MESH)

    for k in range(1, n):
        across(stat, stat_send, stat_recv, k, z).start()

    w_copy(0).wait()
    for tile in range(1, tiles):
        w_copy(tile).start()
    acc[0] = jnp.dot(cen[...], w_s[0], preferred_element_type=jnp.float32).astype(jnp.bfloat16)

    def gat_copy(k):
        return pltpu.make_async_remote_copy(
            src_ref=gat.at[0], dst_ref=gat.at[k], send_sem=gat_send.at[k], recv_sem=gat_recv.at[k],
            device_id=(z, partner(y, k, ny)), device_id_type=MESH)

    def z_copy(stage, index, slot, chunk, to):
        return pltpu.make_async_remote_copy(
            src_ref=stg.at[stage, index], dst_ref=recv.at[slot, chunk % slots], send_sem=send_sem.at[stage, index],
            recv_sem=recv_sem.at[slot, chunk % slots], device_id=(to, y), device_id_type=MESH)

    def arrived(slot, chunk):
        pltpu.make_async_remote_copy(
            src_ref=recv.at[slot, chunk % slots], dst_ref=recv.at[slot, chunk % slots], send_sem=send_sem.at[0, 0],
            recv_sem=recv_sem.at[slot, chunk % slots], device_id=((z + 1) % n, y), device_id_type=MESH).wait_recv()

    def landed(slot, chunk):
        return recv[slot, chunk % slots].astype(jnp.float32)

    def rows(plane):
        return pl.ds(pl.multiple_of(plane * part, part), part)

    def forward(chunk, plane, index, out_slot, in_slot, first, to):
        stage = chunk % stages

        @pl.when(chunk >= stages)
        def _():
            z_copy(stage, index, out_slot, chunk, to).wait_send()

        @pl.when(first)
        def _():
            stg[stage, index] = acc[chunk % ring, rows(plane), :]

        @pl.when(jnp.logical_not(first))
        def _():
            arrived(in_slot, chunk)
            stg[stage, index] = (
                acc[chunk % ring, rows(plane), :].astype(jnp.float32) + landed(in_slot, chunk)
            ).astype(jnp.bfloat16)

        z_copy(stage, index, out_slot, chunk, to).start()

    def right_stage(chunk, j):
        forward(chunk, z + 1 + j, j, j, j + 1, z == 0, z + 1)

    def left_stage(chunk, j):
        forward(chunk, z - 1 - j, n - 2 - j, n - j, n - 1 - j, z == n - 1, z - 1)

    @pl.when(z == 0)
    def _():
        for j in reversed(range(n - 1)):
            right_stage(jnp.int32(0), j)

    @pl.when(z == n - 1)
    def _():
        for j in reversed(range(n - 1)):
            left_stage(jnp.int32(0), j)

    for k in range(1, n):
        across(stat, stat_send, stat_recv, k, (z + n - k) % n).wait_recv()
    sums = [stat[k, 0:1, :] for k in range(n)]
    mean = functools.reduce(lambda a, b: a + b, sums) / model
    spread = jnp.zeros_like(mean)
    for k in range(n):
        shift = sums[k] / depth - mean
        spread = spread + stat[k, 1:2, :] + depth * shift * shift
    rstd = lax.rsqrt(spread / model + EPSILON)
    line = lax.broadcasted_iota(jnp.int32, (128, tok), 0)
    table = jnp.where(line == n, rstd, mean)
    for k in range(n):
        table = jnp.where(line == k, (sums[k] / depth - mean) * rstd, table)
    coef[...] = table.T
    gat[0] = (
        (gat[0].astype(jnp.float32) - coef[:, n + 1:n + 2]) * coef[:, n:n + 1] * gain_row()
    ).astype(jnp.bfloat16)
    for k in range(1, ny):
        gat_copy(k).start()

    block = min(part, max(16, 256 // ny))

    def place(chunk, value):
        group, tile = chunk // tiles, chunk % tiles
        row = lax.broadcasted_iota(jnp.int32, (block * ny, block), 0)
        col = lax.broadcasted_iota(jnp.int32, (block * ny, block), 1)
        take = (row == col * ny + partner(y, group, ny)).astype(jnp.bfloat16)
        for b in range(part // block):
            moved = jnp.dot(
                take, value[b * block:(b + 1) * block], preferred_element_type=jnp.float32).astype(jnp.bfloat16)
            span = slice(b * block * ny, (b + 1) * block * ny)

            @pl.when(group == 0)
            def _():
                out_ref[span, cols(tile)] = moved

            @pl.when(group > 0)
            def _():
                out_ref[span, cols(tile)] += moved

    @pl.loop(1, chunks + n - 1)
    def _(it):
        @pl.when(it < chunks)
        def _():
            tile, group = it % tiles, it // tiles

            @pl.when(group == 0)
            def _():
                w_copy(tile).wait()

            @pl.when(jnp.logical_and(group > 0, tile == 0))
            def _():
                gat_copy(group).wait_recv()

            acc[it % ring] = jnp.dot(gat[group], w_s[tile], preferred_element_type=jnp.float32).astype(jnp.bfloat16)

        for j in reversed(range(n - 1)):
            chunk = it - (n - 2 - j)
            inside = jnp.logical_and(chunk >= 0, chunk < chunks)
            later = jnp.logical_and(chunk >= 1, chunk < chunks)

            @pl.when(jnp.logical_and(z + 1 + j < n, jnp.where(z == 0, later, inside)))
            def _():
                right_stage(chunk, j)

            @pl.when(jnp.logical_and(z - 1 - j >= 0, jnp.where(z == n - 1, later, inside)))
            def _():
                left_stage(chunk, j)

        @pl.when(it == 1)
        def _():
            gain = gain_row()
            high = gain.astype(jnp.bfloat16).astype(jnp.float32)
            term = lax.broadcasted_iota(jnp.int32, (16, depth), 0)
            pair = jnp.where(term == 0, high, jnp.where(term == 1, gain - high, 0.0)).astype(jnp.bfloat16)
            both = jnp.dot(pair, w_s[0], preferred_element_type=jnp.float32)
            gw[z] = both[0:1] + both[1:2]
            for k in range(1, n):
                across(gw, gw_send, gw_recv, k, z).start()

        own = it - (n - 1)

        @pl.when(own == 0)
        def _():
            fin[...] = acc[0, rows(z), :].astype(jnp.float32)

            @pl.when(z > 0)
            def _():
                arrived(0, 0)
                fin[...] += landed(0, 0)

            @pl.when(z < n - 1)
            def _():
                arrived(n, 0)
                fin[...] += landed(n, 0)

            for k in range(1, n):
                across(gw, gw_send, gw_recv, k, (z + n - k) % n).wait_recv()
            mine = coef[rows(z), :]
            value = fin[...] * mine[:, n:n + 1]
            for k in range(n):
                value = value + mine[:, k:k + 1] * gw[k]
            fin[...] = value

        @pl.when(own >= 1)
        def _():
            mine = acc[own % ring, rows(z), :].astype(jnp.float32)

            @pl.when(z == 0)
            def _():
                arrived(n, own)
                fin[...] = mine + landed(n, own)

            @pl.when(z == n - 1)
            def _():
                arrived(0, own)
                fin[...] = mine + landed(0, own)

            @pl.when(jnp.logical_and(z > 0, z < n - 1))
            def _():
                arrived(0, own)
                arrived(n, own)
                fin[...] = mine + landed(0, own) + landed(n, own)

        @pl.when(own >= 0)
        def _():
            place(own, fin[...].astype(jnp.bfloat16))

    for chunk in range(chunks - stages, chunks):
        for index in range(n - 1):
            z_copy(chunk % stages, index, 0, chunk, (z + 1) % n).wait_send()
    for k in range(1, n):
        across(stat, stat_send, stat_recv, k, z).wait_send()
        across(gw, gw_send, gw_recv, k, z).wait_send()
    for k in range(1, ny):
        gat_copy(k).wait_send()


def tile_width(columns, most=7):
    if columns % 128:
        return columns
    lanes = columns // 128
    return 128 * max(k for k in range(1, most + 1) if lanes % k == 0)


def solution(mesh):
    n, ny = mesh.shape["gx"], mesh.shape["gy"]

    def body(tokens, norm_gain, joined_weight):
        tok, depth = tokens.shape
        columns = joined_weight.shape[1]
        part, width = tok // n, tile_width(columns)
        tiles = columns // width
        dma = pltpu.SemaphoreType.DMA
        out = pl.pallas_call(
            functools.partial(kernel, n, ny, width),
            out_shape=pltpu.VMEM((part * ny, columns), jnp.bfloat16),
            in_specs=[pl.BlockSpec(memory_space=pl.ANY)] * 3,
            out_specs=pl.BlockSpec(memory_space=pltpu.VMEM),
            scratch_shapes=[
                pltpu.VMEM((tiles, depth, width), jnp.bfloat16),
                pltpu.VMEM((ny, tok, depth), jnp.bfloat16),
                pltpu.VMEM((depth,), jnp.float32),
                pltpu.VMEM((n, 8, tok), jnp.float32),
                pltpu.VMEM((n + 1, n + 1, part, width), jnp.bfloat16),
                pltpu.VMEM((n, tok, width), jnp.bfloat16),
                pltpu.VMEM((STAGES, n - 1, part, width), jnp.bfloat16),
                pltpu.VMEM((tok, depth), jnp.bfloat16),
                pltpu.VMEM((tok, 128), jnp.float32),
                pltpu.VMEM((n + 8, 1, width), jnp.float32),
                pltpu.VMEM((part, width), jnp.float32),
                dma, dma, dma((tiles,)), dma((n,)), dma((n,)), dma((n,)), dma((n,)),
                dma((ny,)), dma((ny,)),
                dma((STAGES, n - 1)), dma((n + 1, n + 1)),
            ],
            compiler_params=pltpu.CompilerParams(
                collective_id=0, has_side_effects=True, vmem_limit_bytes=58 * 2 ** 20),
        )(tokens, norm_gain, joined_weight)
        return out.reshape(part, ny, columns)

    return jax.shard_map(
        body,
        mesh=mesh,
        in_specs=(P("gy", "gx"), P("gx"), P("gx", "gy")),
        out_specs=P("gx", None, "gy"),
        check_vma=False,
    )
```

time: 384 us -> 366 us (0.953)
  Pallas kernels: 378 us -> 362 us
    pallas_call x2 -> x1, Pallas kernels: 378 us -> 362 us  [body(): pl.pallas_call(functools.partial(kernel, n, ny, width), out_shape=pltpu.V...]
where the time goes in v1:
time: 366 us; the launch traced here: 364 us
  Pallas kernels  362 us (99%)
    pallas_call x1, Pallas kernels, body(): pl.pallas_call(functools.partial(kernel, n, ny, width), out_shape=pltpu.V...  362 us

profile of v1, /device:TPU:8, one launch (start us, length us, event | category | flops | bytes accessed | tf_op | source)
XLA Modules:
  0.0 364.1 jit_solution(18339625877791170499)
XLA Ops:
  0.0 361.7 %shard_map.37 = bf16[512,5376]{1,0:T(8,128)(2,1)S(1)} custom-call(bf16[256,1536]{1,0:T(8,128)(2,1)} %tok_ref.1, f32[1536]{0:T(1024)} %gain_hbm.1, bf16[1536,5376]{1,0:T(8,128)(2,1)} %w_hbm.1), custom_call_target="tpu_custom_call" | custom-call | tf_op jit(solution)/shard_map/pallas_call | solution.py:298
  361.7 2.4 copy.5

commit v2 on v1

--- a/solution.py
+++ b/solution.py
@@ -42,11 +42,19 @@
     def w_copy(tile):
         return pltpu.make_async_copy(w_hbm.at[:, cols(tile)], w_s.at[tile], w_sem.at[tile])
 
+    edges = (0, 256, width) if width > 256 else (0, width)
+    pieces = [slice(lo, hi) for lo, hi in zip(edges, edges[1:])]
+
+    def w_piece(i):
+        return pltpu.make_async_copy(
+            w_hbm.at[:, pieces[i]], w_s.at[0, :, pieces[i]], w_sem.at[tiles if i else 0])
+
     tok_copy = pltpu.make_async_copy(tok_ref, gat.at[0], tok_sem)
     tok_copy.start()
     gain_copy = pltpu.make_async_copy(gain_hbm, gain_s, gain_sem)
     gain_copy.start()
-    w_copy(0).start()
+    for i in range(len(pieces)):
+        w_piece(i).start()
 
     barrier = pltpu.get_barrier_semaphore()
     for k in range(1, n):
@@ -69,21 +77,11 @@
     gain_copy.wait()
     cen[...] = (off * gain_row()).astype(jnp.bfloat16)
 
-    pl.semaphore_wait(barrier, n - 1 + ny - 1)
-
     def across(ref, send, get, k, slot):
         return pltpu.make_async_remote_copy(
             src_ref=ref.at[slot], dst_ref=ref.at[slot], send_sem=send.at[k], recv_sem=get.at[k],
             device_id=((z + k) % n, y), device_id_type=MESH)
 
-    for k in range(1, n):
-        across(stat, stat_send, stat_recv, k, z).start()
-
-    w_copy(0).wait()
-    for tile in range(1, tiles):
-        w_copy(tile).start()
-    acc[0] = jnp.dot(cen[...], w_s[0], preferred_element_type=jnp.float32).astype(jnp.bfloat16)
-
     def gat_copy(k):
         return pltpu.make_async_remote_copy(
             src_ref=gat.at[0], dst_ref=gat.at[k], send_sem=gat_send.at[k], recv_sem=gat_recv.at[k],
@@ -131,15 +129,35 @@
     def left_stage(chunk, j):
         forward(chunk, z - 1 - j, n - 2 - j, n - j, n - 1 - j, z == n - 1, z - 1)
 
-    @pl.when(z == 0)
-    def _():
-        for j in reversed(range(n - 1)):
-            right_stage(jnp.int32(0), j)
-
-    @pl.when(z == n - 1)
-    def _():
-        for j in reversed(range(n - 1)):
-            left_stage(jnp.int32(0), j)
+    def open_stage(plane, index, slot, piece, to):
+        stg[0, index, :, piece] = acc[0, rows(plane), piece]
+        pltpu.make_async_remote_copy(
+            src_ref=stg.at[0, index, :, piece], dst_ref=recv.at[slot, 0, :, piece], send_sem=send_sem.at[0, index],
+            recv_sem=recv_sem.at[slot, 0], device_id=(to, y), device_id_type=MESH).start()
+
+    for i, piece in enumerate(pieces):
+        w_piece(i).wait()
+        if i == len(pieces) - 1:
+            for tile in range(1, tiles):
+                w_copy(tile).start()
+        acc[0, :, piece] = jnp.dot(
+            cen[...], w_s[0, :, piece], preferred_element_type=jnp.float32).astype(jnp.bfloat16)
+        if i == 0:
+            pl.semaphore_wait(barrier, n - 1 + ny - 1)
+
+        @pl.when(z == 0)
+        def _():
+            for j in reversed(range(n - 1)):
+                open_stage(1 + j, j, j, piece, 1)
+
+        @pl.when(z == n - 1)
+        def _():
+            for j in reversed(range(n - 1)):
+                open_stage(n - 2 - j, n - 2 - j, n - j, piece, n - 2)
+
+        if i == 0:
+            for k in range(1, n):
+                across(stat, stat_send, stat_recv, k, z).start()
 
     for k in range(1, n):
         across(stat, stat_send, stat_recv, k, (z + n - k) % n).wait_recv()
@@ -202,11 +220,17 @@
             inside = jnp.logical_and(chunk >= 0, chunk < chunks)
             later = jnp.logical_and(chunk >= 1, chunk < chunks)
 
+            left = jnp.logical_and(z - 1 - j >= 0, jnp.where(z == n - 1, later, inside))
+
+            @pl.when(jnp.logical_and(left, 2 * z < n))
+            def _():
+                left_stage(chunk, j)
+
             @pl.when(jnp.logical_and(z + 1 + j < n, jnp.where(z == 0, later, inside)))
             def _():
                 right_stage(chunk, j)
 
-            @pl.when(jnp.logical_and(z - 1 - j >= 0, jnp.where(z == n - 1, later, inside)))
+            @pl.when(jnp.logical_and(left, 2 * z >= n))
             def _():
                 left_stage(chunk, j)
 
@@ -312,7 +336,7 @@
                 pltpu.VMEM((tok, 128), jnp.float32),
                 pltpu.VMEM((n + 8, 1, width), jnp.float32),
                 pltpu.VMEM((part, width), jnp.float32),
-                dma, dma, dma((tiles,)), dma((n,)), dma((n,)), dma((n,)), dma((n,)),
+                dma, dma, dma((tiles + 1,)), dma((n,)), dma((n,)), dma((n,)), dma((n,)),
                 dma((ny,)), dma((ny,)),
                 dma((STAGES, n - 1)), dma((n + 1, n + 1)),
             ],

time: 366 us -> 364 us (level)
  no operation moved by 1% of the time
where the time goes in v2:
time: 364 us
  Pallas kernels  361 us (99%)
    pallas_call x1, Pallas kernels, body(): pl.pallas_call(functools.partial(kernel, n, ny, width), out_shape=pltpu.V...  361 us

profile of v2, /device:TPU:8, one launch (start us, length us, event | category | flops | bytes accessed | tf_op | source)
XLA Modules:
  0.0 363.7 jit_solution(15053685652132144614)
XLA Ops:
  0.0 361.2 %shard_map.37 = bf16[512,5376]{1,0:T(8,128)(2,1)S(1)} custom-call(bf16[256,1536]{1,0:T(8,128)(2,1)} %tok_ref.1, f32[1536]{0:T(1024)} %gain_hbm.1, bf16[1536,5376]{1,0:T(8,128)(2,1)} %w_hbm.1), custom_call_target="tpu_custom_call" | custom-call | tf_op jit(solution)/shard_map/pallas_call | solution.py:322
  361.2 2.4 copy.5

commit v3 on v2

--- a/solution.py
+++ b/solution.py
@@ -10,6 +10,7 @@
 MESH = pl.DeviceIdType.MESH
 EPSILON = 1e-06
 STAGES = 4
+EARLY = 2
 
 
 def partner(y, step, ny):
@@ -22,7 +23,7 @@
 
 def kernel(n, ny, width, tok_ref, gain_hbm, w_hbm, out_ref, w_s, gat, gain_s, stat, recv, acc, stg,
            cen, coef, gw, fin, tok_sem, gain_sem, w_sem, stat_send, stat_recv, gw_send, gw_recv, gat_send, gat_recv,
-           send_sem, recv_sem):
+           send_sem, recv_sem, met):
     z, y = lax.axis_index("gx"), lax.axis_index("gy")
     tok, depth = tok_ref.shape
     part = tok // n
@@ -34,48 +35,56 @@
     ring = acc.shape[0]
     model = depth * n
 
-    def cols(tile):
+    def cols(tile, piece=slice(0, width)):
         if tiles == 1:
-            return slice(None)
-        return pl.ds(pl.multiple_of(tile * width, 128), width)
+            return piece
+        return pl.ds(pl.multiple_of(tile * width + piece.start, 128), piece.stop - piece.start)
 
     def w_copy(tile):
         return pltpu.make_async_copy(w_hbm.at[:, cols(tile)], w_s.at[tile], w_sem.at[tile])
 
-    edges = (0, 256, width) if width > 256 else (0, width)
+    edges = (0, 384, width) if width > 384 else (0, width)
     pieces = [slice(lo, hi) for lo, hi in zip(edges, edges[1:])]
 
     def w_piece(i):
         return pltpu.make_async_copy(
             w_hbm.at[:, pieces[i]], w_s.at[0, :, pieces[i]], w_sem.at[tiles if i else 0])
 
-    tok_copy = pltpu.make_async_copy(tok_ref, gat.at[0], tok_sem)
-    tok_copy.start()
+    def rows(plane):
+        return pl.ds(pl.multiple_of(plane * part, part), part)
+
+    order = [jnp.where(2 * z < n, n - 1 - i, i) for i in range(n)]
+
+    def tok_copy(i):
+        return pltpu.make_async_copy(tok_ref.at[rows(order[i])], gat.at[0, rows(order[i])], tok_sem.at[i])
+
+    for i in range(n):
+        tok_copy(i).start()
     gain_copy = pltpu.make_async_copy(gain_hbm, gain_s, gain_sem)
     gain_copy.start()
     for i in range(len(pieces)):
         w_piece(i).start()
 
+    bits = (ny - 1).bit_length()
+    degree = (z > 0).astype(jnp.int32) + (z < n - 1).astype(jnp.int32) + bits
+
+    def greet(sem):
+        @pl.when(z > 0)
+        def _():
+            pl.semaphore_signal(sem, inc=1, device_id=(z - 1, y), device_id_type=MESH)
+
+        @pl.when(z < n - 1)
+        def _():
+            pl.semaphore_signal(sem, inc=1, device_id=(z + 1, y), device_id_type=MESH)
+
+        for bit in range(bits):
+            pl.semaphore_signal(sem, inc=1, device_id=(z, partner(y, 1 << bit, ny)), device_id_type=MESH)
+
     barrier = pltpu.get_barrier_semaphore()
-    for k in range(1, n):
-        pl.semaphore_signal(barrier, inc=1, device_id=((z + k) % n, y), device_id_type=MESH)
-    for k in range(1, ny):
-        pl.semaphore_signal(barrier, inc=1, device_id=(z, partner(y, k, ny)), device_id_type=MESH)
+    greet(barrier)
 
     def gain_row():
         return gain_s[...].reshape(1, depth)
-
-    tok_copy.wait()
-    values = gat[0].astype(jnp.float32)
-    total = jnp.sum(values, axis=1, keepdims=True)
-    off = values - total / depth
-    squares = jnp.sum(off * off, axis=1, keepdims=True)
-    lane = lax.broadcasted_iota(jnp.int32, (tok, 128), 1)
-    packed = jnp.where(lane == 0, total, squares)
-    stat[z] = packed.T[:8]
-
-    gain_copy.wait()
-    cen[...] = (off * gain_row()).astype(jnp.bfloat16)
 
     def across(ref, send, get, k, slot):
         return pltpu.make_async_remote_copy(
@@ -92,6 +101,16 @@
             src_ref=stg.at[stage, index], dst_ref=recv.at[slot, chunk % slots], send_sem=send_sem.at[stage, index],
             recv_sem=recv_sem.at[slot, chunk % slots], device_id=(to, y), device_id_type=MESH)
 
+    last = chunks - 1
+    cut = (width - 256) // 128 * 128
+    ends = [slice(0, cut), slice(cut, width)] if cut > 0 else [slice(0, width)]
+
+    def end_copy(index, slot, i, to):
+        return pltpu.make_async_remote_copy(
+            src_ref=stg.at[last % stages, index, :, ends[i]], dst_ref=recv.at[slot, last % slots, :, ends[i]],
+            send_sem=send_sem.at[last % stages, index], recv_sem=recv_sem.at[slot, slots if i else last % slots],
+            device_id=(to, y), device_id_type=MESH)
+
     def arrived(slot, chunk):
         pltpu.make_async_remote_copy(
             src_ref=recv.at[slot, chunk % slots], dst_ref=recv.at[slot, chunk % slots], send_sem=send_sem.at[0, 0],
@@ -100,10 +119,7 @@
     def landed(slot, chunk):
         return recv[slot, chunk % slots].astype(jnp.float32)
 
-    def rows(plane):
-        return pl.ds(pl.multiple_of(plane * part, part), part)
-
-    def forward(chunk, plane, index, out_slot, in_slot, first, to):
+    def forward(chunk, plane, index, out_slot, in_slot, first, to, whole):
         stage = chunk % stages
 
         @pl.when(chunk >= stages)
@@ -121,13 +137,17 @@
                 acc[chunk % ring, rows(plane), :].astype(jnp.float32) + landed(in_slot, chunk)
             ).astype(jnp.bfloat16)
 
-        z_copy(stage, index, out_slot, chunk, to).start()
-
-    def right_stage(chunk, j):
-        forward(chunk, z + 1 + j, j, j, j + 1, z == 0, z + 1)
-
-    def left_stage(chunk, j):
-        forward(chunk, z - 1 - j, n - 2 - j, n - j, n - 1 - j, z == n - 1, z - 1)
+        if whole:
+            z_copy(stage, index, out_slot, chunk, to).start()
+        else:
+            for i in range(len(ends)):
+                end_copy(index, out_slot, i, to).start()
+
+    def right_stage(chunk, j, whole=True):
+        forward(chunk, z + 1 + j, j, j, j + 1, z == 0, z + 1, whole)
+
+    def left_stage(chunk, j, whole=True):
+        forward(chunk, z - 1 - j, n - 2 - j, n - j, n - 1 - j, z == n - 1, z - 1, whole)
 
     def open_stage(plane, index, slot, piece, to):
         stg[0, index, :, piece] = acc[0, rows(plane), piece]
@@ -135,15 +155,54 @@
             src_ref=stg.at[0, index, :, piece], dst_ref=recv.at[slot, 0, :, piece], send_sem=send_sem.at[0, index],
             recv_sem=recv_sem.at[slot, 0], device_id=(to, y), device_id_type=MESH).start()
 
-    for i, piece in enumerate(pieces):
-        w_piece(i).wait()
-        if i == len(pieces) - 1:
-            for tile in range(1, tiles):
-                w_copy(tile).start()
+    gain_copy.wait()
+    lane = lax.broadcasted_iota(jnp.int32, (part, 128), 1)
+    for i in range(n):
+        mine = rows(order[i])
+        tok_copy(i).wait()
+        values = gat[0, mine, :].astype(jnp.float32)
+        total = jnp.sum(values, axis=1, keepdims=True)
+        off = values - total / depth
+        squares = jnp.sum(off * off, axis=1, keepdims=True)
+        coef[mine, :] = jnp.where(lane == 0, total, squares)
+        cen[mine, :] = (off * gain_row()).astype(jnp.bfloat16)
+        if i == 0:
+            w_piece(0).wait()
+        acc[0, mine, pieces[0]] = jnp.dot(
+            cen[mine, :], w_s[0, :, pieces[0]], preferred_element_type=jnp.float32).astype(jnp.bfloat16)
+        if i == 0:
+            pl.semaphore_wait(barrier, degree)
+            greet(met.at[0])
+        if i < n - 1:
+            @pl.when(z == 0)
+            def _():
+                open_stage(n - 1 - i, n - 2 - i, n - 2 - i, pieces[0], 1)
+
+            @pl.when(z == n - 1)
+            def _():
+                open_stage(i, i, i + 2, pieces[0], n - 2)
+
+    def near(k):
+        return jnp.abs((z + k) % n - z) == 1
+
+    stat[z] = coef[...].T[:8]
+    for k in range(1, n):
+        @pl.when(near(k))
+        def _():
+            across(stat, stat_send, stat_recv, k, z).start()
+
+    rounds = met.shape[0]
+    for r in range(1, rounds):
+        pl.semaphore_wait(met.at[r - 1], degree)
+        greet(met.at[r])
+
+    if len(pieces) > 1:
+        w_piece(1).wait()
+    for tile in range(1, tiles):
+        w_copy(tile).start()
+    for piece in pieces[1:]:
         acc[0, :, piece] = jnp.dot(
             cen[...], w_s[0, :, piece], preferred_element_type=jnp.float32).astype(jnp.bfloat16)
-        if i == 0:
-            pl.semaphore_wait(barrier, n - 1 + ny - 1)
 
         @pl.when(z == 0)
         def _():
@@ -155,9 +214,37 @@
             for j in reversed(range(n - 1)):
                 open_stage(n - 2 - j, n - 2 - j, n - j, piece, n - 2)
 
-        if i == 0:
-            for k in range(1, n):
-                across(stat, stat_send, stat_recv, k, z).start()
+    pl.semaphore_wait(met.at[rounds - 1], degree)
+    for k in range(1, n):
+        @pl.when(jnp.logical_not(near(k)))
+        def _():
+            across(stat, stat_send, stat_recv, k, z).start()
+
+    early = min(EARLY, tiles)
+    gain = gain_row()
+    high = gain.astype(jnp.bfloat16).astype(jnp.float32)
+    term = lax.broadcasted_iota(jnp.int32, (16, depth), 0)
+    pair = jnp.where(term == 0, high, jnp.where(term == 1, gain - high, 0.0)).astype(jnp.bfloat16)
+    for tile in range(early):
+        if tile > 0:
+            w_copy(tile).wait()
+        both = jnp.dot(pair, w_s[tile], preferred_element_type=jnp.float32)
+        gw[z, :, tile * width:(tile + 1) * width] = both[0:1] + both[1:2]
+    for k in range(1, n):
+        across(gw, gw_send, gw_recv, k, z).start()
+
+    for tile in range(1, early):
+        acc[tile] = jnp.dot(cen[...], w_s[tile], preferred_element_type=jnp.float32).astype(jnp.bfloat16)
+
+        @pl.when(z == 0)
+        def _():
+            for j in reversed(range(n - 1)):
+                right_stage(jnp.int32(tile), j)
+
+        @pl.when(z == n - 1)
+        def _():
+            for j in reversed(range(n - 1)):
+                left_stage(jnp.int32(tile), j)
 
     for k in range(1, n):
         across(stat, stat_send, stat_recv, k, (z + n - k) % n).wait_recv()
@@ -181,7 +268,7 @@
 
     block = min(part, max(16, 256 // ny))
 
-    def place(chunk, value):
+    def place(chunk, value, piece=slice(0, width)):
         group, tile = chunk // tiles, chunk % tiles
         row = lax.broadcasted_iota(jnp.int32, (block * ny, block), 0)
         col = lax.broadcasted_iota(jnp.int32, (block * ny, block), 1)
@@ -193,15 +280,37 @@
 
             @pl.when(group == 0)
             def _():
-                out_ref[span, cols(tile)] = moved
+                out_ref[span, cols(tile, piece)] = moved
 
             @pl.when(group > 0)
             def _():
-                out_ref[span, cols(tile)] += moved
-
-    @pl.loop(1, chunks + n - 1)
+                out_ref[span, cols(tile, piece)] += moved
+
+    def settle(chunk, wait, piece=slice(0, width)):
+        mine = acc[chunk % ring, rows(z), piece].astype(jnp.float32)
+
+        def there(slot):
+            return recv[slot, chunk % slots, :, piece].astype(jnp.float32)
+
+        @pl.when(z == 0)
+        def _():
+            wait(n)
+            fin[:, piece] = mine + there(n)
+
+        @pl.when(z == n - 1)
+        def _():
+            wait(0)
+            fin[:, piece] = mine + there(0)
+
+        @pl.when(jnp.logical_and(z > 0, z < n - 1))
+        def _():
+            wait(0)
+            wait(n)
+            fin[:, piece] = mine + there(0) + there(n)
+
+    @pl.loop(1, chunks + n - 3)
     def _(it):
-        @pl.when(it < chunks)
+        @pl.when(jnp.logical_and(it >= early, it < chunks))
         def _():
             tile, group = it % tiles, it // tiles
 
@@ -218,7 +327,7 @@
         for j in reversed(range(n - 1)):
             chunk = it - (n - 2 - j)
             inside = jnp.logical_and(chunk >= 0, chunk < chunks)
-            later = jnp.logical_and(chunk >= 1, chunk < chunks)
+            later = jnp.logical_and(chunk >= early, chunk < chunks)
 
             left = jnp.logical_and(z - 1 - j >= 0, jnp.where(z == n - 1, later, inside))
 
@@ -234,64 +343,45 @@
             def _():
                 left_stage(chunk, j)
 
-        @pl.when(it == 1)
-        def _():
-            gain = gain_row()
-            high = gain.astype(jnp.bfloat16).astype(jnp.float32)
-            term = lax.broadcasted_iota(jnp.int32, (16, depth), 0)
-            pair = jnp.where(term == 0, high, jnp.where(term == 1, gain - high, 0.0)).astype(jnp.bfloat16)
-            both = jnp.dot(pair, w_s[0], preferred_element_type=jnp.float32)
-            gw[z] = both[0:1] + both[1:2]
-            for k in range(1, n):
-                across(gw, gw_send, gw_recv, k, z).start()
-
         own = it - (n - 1)
 
-        @pl.when(own == 0)
-        def _():
-            fin[...] = acc[0, rows(z), :].astype(jnp.float32)
-
-            @pl.when(z > 0)
-            def _():
-                arrived(0, 0)
-                fin[...] += landed(0, 0)
-
-            @pl.when(z < n - 1)
-            def _():
-                arrived(n, 0)
-                fin[...] += landed(n, 0)
-
-            for k in range(1, n):
-                across(gw, gw_send, gw_recv, k, (z + n - k) % n).wait_recv()
-            mine = coef[rows(z), :]
-            value = fin[...] * mine[:, n:n + 1]
-            for k in range(n):
-                value = value + mine[:, k:k + 1] * gw[k]
-            fin[...] = value
-
-        @pl.when(own >= 1)
-        def _():
-            mine = acc[own % ring, rows(z), :].astype(jnp.float32)
-
-            @pl.when(z == 0)
-            def _():
-                arrived(n, own)
-                fin[...] = mine + landed(n, own)
-
-            @pl.when(z == n - 1)
-            def _():
-                arrived(0, own)
-                fin[...] = mine + landed(0, own)
-
-            @pl.when(jnp.logical_and(z > 0, z < n - 1))
-            def _():
-                arrived(0, own)
-                arrived(n, own)
-                fin[...] = mine + landed(0, own) + landed(n, own)
-
         @pl.when(own >= 0)
         def _():
+            settle(own, lambda slot: arrived(slot, own))
+
+        for tile in range(early):
+            @pl.when(own == tile)
+            def _():
+                if tile == 0:
+                    for k in range(1, n):
+                        across(gw, gw_send, gw_recv, k, (z + n - k) % n).wait_recv()
+                mine = coef[rows(z), :]
+                value = fin[...] * mine[:, n:n + 1]
+                for k in range(n):
+                    value = value + mine[:, k:k + 1] * gw[k, :, tile * width:(tile + 1) * width]
+                fin[...] = value
+
+        @pl.when(own >= 0)
+        def _():
             place(own, fin[...].astype(jnp.bfloat16))
+
+    @pl.when(jnp.logical_and(z > 0, 2 * z < n))
+    def _():
+        left_stage(last, 0, False)
+
+    @pl.when(z < n - 1)
+    def _():
+        right_stage(last, 0, False)
+
+    @pl.when(2 * z >= n)
+    def _():
+        left_stage(last, 0, False)
+
+    settle(last - 1, lambda slot: arrived(slot, last - 1))
+    place(last - 1, fin[...].astype(jnp.bfloat16))
+    for i, piece in enumerate(ends):
+        settle(last, lambda slot: end_copy(0, slot, i, (z + 1) % n).wait_recv(), piece)
+        place(last, fin[:, piece].astype(jnp.bfloat16), piece)
 
     for chunk in range(chunks - stages, chunks):
         for index in range(n - 1):
@@ -334,11 +424,12 @@
                 pltpu.VMEM((STAGES, n - 1, part, width), jnp.bfloat16),
                 pltpu.VMEM((tok, depth), jnp.bfloat16),
                 pltpu.VMEM((tok, 128), jnp.float32),
-                pltpu.VMEM((n + 8, 1, width), jnp.float32),
+                pltpu.VMEM((n + 8, 1, min(EARLY, tiles) * width), jnp.float32),
                 pltpu.VMEM((part, width), jnp.float32),
-                dma, dma, dma((tiles + 1,)), dma((n,)), dma((n,)), dma((n,)), dma((n,)),
+                dma((n,)), dma, dma((tiles + 1,)), dma((n,)), dma((n,)), dma((n,)), dma((n,)),
                 dma((ny,)), dma((ny,)),
-                dma((STAGES, n - 1)), dma((n + 1, n + 1)),
+                dma((STAGES, n - 1)), dma((n + 1, n + 2)),
+                pltpu.SemaphoreType.REGULAR((max(n - 1, (ny - 1).bit_length()) - 1,)),
             ],
             compiler_params=pltpu.CompilerParams(
                 collective_id=0, has_side_effects=True, vmem_limit_bytes=58 * 2 ** 20),

time: 364 us -> 363 us (level)
  no operation moved by 1% of the time
where the time goes in v3:
time: 363 us
  Pallas kernels  360 us (99%)
    pallas_call x1, Pallas kernels, body(): pl.pallas_call(functools.partial(kernel, n, ny, width), out_shape=pltpu.V...  360 us

profile of v3, /device:TPU:8, one launch (start us, length us, event | category | flops | bytes accessed | tf_op | source)
XLA Modules:
  0.0 362.9 jit_solution(3143779385774844616)
XLA Ops:
  0.0 360.4 %shard_map.37 = bf16[512,5376]{1,0:T(8,128)(2,1)S(1)} custom-call(bf16[256,1536]{1,0:T(8,128)(2,1)} %tok_ref.1, f32[1536]{0:T(1024)} %gain_hbm.1, bf16[1536,5376]{1,0:T(8,128)(2,1)} %w_hbm.1), custom_call_target="tpu_custom_call" | custom-call | tf_op jit(solution)/shard_map/pallas_call | solution.py:412
  360.4 2.4 copy.5

commit v4 on v3

--- a/solution.py
+++ b/solution.py
@@ -62,8 +62,7 @@
         tok_copy(i).start()
     gain_copy = pltpu.make_async_copy(gain_hbm, gain_s, gain_sem)
     gain_copy.start()
-    for i in range(len(pieces)):
-        w_piece(i).start()
+    w_piece(0).start()
 
     bits = (ny - 1).bit_length()
     degree = (z > 0).astype(jnp.int32) + (z < n - 1).astype(jnp.int32) + bits
@@ -160,6 +159,8 @@
     for i in range(n):
         mine = rows(order[i])
         tok_copy(i).wait()
+        if i == 0 and len(pieces) > 1:
+            w_piece(1).start()
         values = gat[0, mine, :].astype(jnp.float32)
         total = jnp.sum(values, axis=1, keepdims=True)
         off = values - total / depth
@@ -185,7 +186,7 @@
     def near(k):
         return jnp.abs((z + k) % n - z) == 1
 
-    stat[z] = coef[...].T[:8]
+    stat[z] = coef[...].T[:2]
     for k in range(1, n):
         @pl.when(near(k))
         def _():
@@ -230,8 +231,31 @@
             w_copy(tile).wait()
         both = jnp.dot(pair, w_s[tile], preferred_element_type=jnp.float32)
         gw[z, :, tile * width:(tile + 1) * width] = both[0:1] + both[1:2]
-    for k in range(1, n):
-        across(gw, gw_send, gw_recv, k, z).start()
+    def gw_copy(source, side):
+        return pltpu.make_async_remote_copy(
+            src_ref=gw.at[source], dst_ref=gw.at[source], send_sem=gw_send.at[side, source],
+            recv_sem=gw_recv.at[source], device_id=(z + 1 if side else z - 1, y), device_id_type=MESH)
+
+    def to_right(hop):
+        return jnp.logical_and(z >= hop, z < n - 1)
+
+    def to_left(hop):
+        return jnp.logical_and(z + hop < n, z > 0)
+
+    def hand_on(hop):
+        @pl.when(to_right(hop))
+        def _():
+            if hop > 0:
+                gw_copy(z - hop, 1).wait_recv()
+            gw_copy(z - hop, 1).start()
+
+        @pl.when(to_left(hop))
+        def _():
+            if hop > 0:
+                gw_copy(z + hop, 0).wait_recv()
+            gw_copy(z + hop, 0).start()
+
+    hand_on(0)
 
     for tile in range(1, early):
         acc[tile] = jnp.dot(cen[...], w_s[tile], preferred_element_type=jnp.float32).astype(jnp.bfloat16)
@@ -353,8 +377,16 @@
             @pl.when(own == tile)
             def _():
                 if tile == 0:
-                    for k in range(1, n):
-                        across(gw, gw_send, gw_recv, k, (z + n - k) % n).wait_recv()
+                    @pl.when(z == 0)
+                    def _():
+                        for k in range(1, n):
+                            gw_copy(k, 1).wait_recv()
+
+                    @pl.when(z == n - 1)
+                    def _():
+                        for k in range(n - 1):
+                            gw_copy(k, 0).wait_recv()
+
                 mine = coef[rows(z), :]
                 value = fin[...] * mine[:, n:n + 1]
                 for k in range(n):
@@ -365,6 +397,11 @@
         def _():
             place(own, fin[...].astype(jnp.bfloat16))
 
+        for hop in range(1, n - 1):
+            @pl.when(it == hop)
+            def _():
+                hand_on(hop)
+
     @pl.when(jnp.logical_and(z > 0, 2 * z < n))
     def _():
         left_stage(last, 0, False)
@@ -388,7 +425,15 @@
             z_copy(chunk % stages, index, 0, chunk, (z + 1) % n).wait_send()
     for k in range(1, n):
         across(stat, stat_send, stat_recv, k, z).wait_send()
-        across(gw, gw_send, gw_recv, k, z).wait_send()
+    for hop in range(n - 1):
+        @pl.when(to_right(hop))
+        def _():
+            gw_copy(z - hop, 1).wait_send()
+
+        @pl.when(to_left(hop))
+        def _():
+            gw_copy(z + hop, 0).wait_send()
+
     for k in range(1, ny):
         gat_copy(k).wait_send()
 
@@ -418,7 +463,7 @@
                 pltpu.VMEM((tiles, depth, width), jnp.bfloat16),
                 pltpu.VMEM((ny, tok, depth), jnp.bfloat16),
                 pltpu.VMEM((depth,), jnp.float32),
-                pltpu.VMEM((n, 8, tok), jnp.float32),
+                pltpu.VMEM((n + 8, 2, tok), jnp.float32),
                 pltpu.VMEM((n + 1, n + 1, part, width), jnp.bfloat16),
                 pltpu.VMEM((n, tok, width), jnp.bfloat16),
                 pltpu.VMEM((STAGES, n - 1, part, width), jnp.bfloat16),
@@ -426,7 +471,7 @@
                 pltpu.VMEM((tok, 128), jnp.float32),
                 pltpu.VMEM((n + 8, 1, min(EARLY, tiles) * width), jnp.float32),
                 pltpu.VMEM((part, width), jnp.float32),
-                dma((n,)), dma, dma((tiles + 1,)), dma((n,)), dma((n,)), dma((n,)), dma((n,)),
+                dma((n,)), dma, dma((tiles + 1,)), dma((n,)), dma((n,)), dma((2, n)), dma((n,)),
                 dma((ny,)), dma((ny,)),
                 dma((STAGES, n - 1)), dma((n + 1, n + 2)),
                 pltpu.SemaphoreType.REGULAR((max(n - 1, (ny - 1).bit_length()) - 1,)),

time: 363 us -> 362 us (level)
  no operation moved by 1% of the time
where the time goes in v4:
time: 362 us
  Pallas kernels  360 us (99%)
    pallas_call x1, Pallas kernels, body(): pl.pallas_call(functools.partial(kernel, n, ny, width), out_shape=pltpu.V...  360 us

profile of v4, /device:TPU:8, one launch (start us, length us, event | category | flops | bytes accessed | tf_op | source)
XLA Modules:
  0.0 362.2 jit_solution(14766170355219215630)
XLA Ops:
  0.0 359.8 %shard_map.37 = bf16[512,5376]{1,0:T(8,128)(2,1)S(1)} custom-call(bf16[256,1536]{1,0:T(8,128)(2,1)} %tok_ref.1, f32[1536]{0:T(1024)} %gain_hbm.1, bf16[1536,5376]{1,0:T(8,128)(2,1)} %w_hbm.1), custom_call_target="tpu_custom_call" | custom-call | tf_op jit(solution)/shard_map/pallas_call | solution.py:457
  359.8 2.4 copy.5

commit v5 on v4

--- a/solution.py
+++ b/solution.py
@@ -9,7 +9,7 @@
 
 MESH = pl.DeviceIdType.MESH
 EPSILON = 1e-06
-STAGES = 4
+STAGES = 6
 EARLY = 2
 
 

time: 362 us -> 362 us (level)
  no operation moved by 1% of the time
where the time goes in v5:
time: 362 us
  Pallas kernels  360 us (99%)
    pallas_call x1, Pallas kernels, body(): pl.pallas_call(functools.partial(kernel, n, ny, width), out_shape=pltpu.V...  360 us

profile of v5, /device:TPU:8, one launch (start us, length us, event | category | flops | bytes accessed | tf_op | source)
XLA Modules:
  0.0 362.3 jit_solution(17202512769639498458)
XLA Ops:
  0.0 359.8 %shard_map.37 = bf16[512,5376]{1,0:T(8,128)(2,1)S(1)} custom-call(bf16[256,1536]{1,0:T(8,128)(2,1)} %tok_ref.1, f32[1536]{0:T(1024)} %gain_hbm.1, bf16[1536,5376]{1,0:T(8,128)(2,1)} %w_hbm.1), custom_call_target="tpu_custom_call" | custom-call | tf_op jit(solution)/shard_map/pallas_call | solution.py:457
  359.8 2.4 copy.5
